TPU v7x, 32 devices: a whole 2x2x4 slice. The times are simulated.
32 devices in a mesh: sub: 16 (over z, y, core), tm: 2 (over x).
Axes of the slice: x: 2, y: 2, z: 4, core: 2. Of those that a mesh axis runs over, the one named last changes fastest.
Arguments:
- voltages: bfloat16 [192, 2, 96, 2048], P('sub', None, None, 'tm'), may hold values from -6 to 6
- pointing_table: bfloat16 [192, 2, 320, 96], P('sub'), may hold values from -0.4375 to 0.4375
- beam_pointing: int32 [256], replicated, may hold values from 0 to 319
- subband_order: int32 [192], replicated, may hold values from 0 to 191, each once
- live_subbands: int32 [1], replicated, may hold values from 152 to 192
- filter_taps: float32 [16, 16], replicated, may hold values from -0.36 to 0.36
Outputs:
- synthesised: bfloat16 [256, 12, 2, 32768], P('sub', None, None, 'tm')
Inputs may be any that keep to these rules, and one draw needn't show every extreme that they name: `subband_order`: each slot is named by exactly one frequency.
All inputs are finite; a program needn't handle non-finite values.
Results may differ from a plain program's by a relative error of at most 0.0052.
Values may be sent and summed in bfloat16 or wider, within the bound.
A program may use at most 192 MiB of HBM per device.

v0:
```python
import math

import jax
import jax.numpy as jnp
from jax import lax
from jax.sharding import PartitionSpec as P


def shifted(block, axis, distance):
    devices = range(lax.axis_size(axis))
    route = [(i - distance, i) for i in devices if i - distance in devices]
    return lax.ppermute(block, axis, route)


def inverse_table(channel_count):
    channel_index = jnp.arange(channel_count, dtype=jnp.int32)
    phase = (jnp.outer(channel_index, channel_index) % channel_count).astype(jnp.float32) * (
        2.0 * math.pi / channel_count
    )
    cosine = jnp.cos(phase).astype(jnp.bfloat16)
    sine_table = jnp.sin(phase).astype(jnp.bfloat16)
    upper_rows = jnp.stack([cosine, -sine_table], axis=1)
    lower_rows = jnp.stack([sine_table, cosine], axis=1)
    return jnp.stack([upper_rows, lower_rows], axis=0)


def spectrum_channels(beam_rows, subband_order, live_subbands, inverse_rows):
    slot_count = beam_rows.shape[0]
    channel_count = inverse_rows.shape[1]
    spectrum = jnp.take(beam_rows, subband_order, axis=0)
    live_mask = jnp.arange(slot_count, dtype=jnp.int32) < live_subbands[0]
    spectrum = jnp.where(live_mask[:, None, None, None], spectrum, jnp.zeros_like(spectrum))
    grouped = spectrum.reshape(
        slot_count // channel_count, channel_count, beam_rows.shape[1], 2, beam_rows.shape[3]
    )
    channels = jnp.einsum(
        "qkpc,gcbpt->bgqkt", inverse_rows, grouped, preferred_element_type=jnp.float32
    )
    return (grouped, channels)


def polyphase(channels, earlier, filter_taps):
    length = channels.shape[4]
    tap_count = filter_taps.shape[0]
    extended = jnp.concatenate([earlier, channels], axis=4)
    running = jnp.zeros_like(channels)
    for tap_index in range(tap_count):
        offset = tap_count - 1 - tap_index
        running = (
            running + filter_taps[tap_index][:, None] * extended[..., offset : offset + length]
        )
    channel_shape = channels.shape
    return (
        jnp.swapaxes(running, 3, 4)
        .reshape(channel_shape[0], channel_shape[1], 2, length * channel_shape[3])
        .astype(jnp.bfloat16)
    )


def on_device(voltages, pointing_table, beam_pointing, subband_order, live_subbands, filter_taps):
    local_subbands = voltages.shape[0]
    inputs = voltages.shape[2]
    local_time = voltages.shape[3]
    beam_count = beam_pointing.shape[0]
    rim_width = filter_taps.shape[0] - 1
    chosen = jnp.take(pointing_table, beam_pointing, axis=2)
    real_weight = chosen[:, 0]
    imag_weight = chosen[:, 1]
    stacked = jnp.stack(
        [
            jnp.concatenate([real_weight, -imag_weight], axis=2),
            jnp.concatenate([imag_weight, real_weight], axis=2),
        ],
        axis=2,
    )
    stacked = stacked.reshape(local_subbands, 2 * beam_count, 2 * inputs)
    signal = voltages.reshape(local_subbands, 2 * inputs, local_time)
    formed = jnp.einsum("sqi,sit->sqt", stacked, signal, preferred_element_type=jnp.float32).astype(
        jnp.bfloat16
    )
    inverse_rows = inverse_table(filter_taps.shape[1])
    axis_devices = lax.axis_size("sub")
    beam_part = beam_count // axis_devices
    blocks = formed.reshape(local_subbands, axis_devices, beam_part, 2, local_time)
    beam_rows = lax.all_to_all(blocks, "sub", split_axis=1, concat_axis=0, tiled=True)[:, 0]
    grouped, channels = spectrum_channels(beam_rows, subband_order, live_subbands, inverse_rows)
    earlier = shifted(channels[..., local_time - rim_width :].astype(jnp.bfloat16), "tm", 1).astype(
        jnp.float32
    )
    return polyphase(channels, earlier, filter_taps)


def solution(mesh):
    in_specs = (P("sub", None, None, "tm"), P("sub", None, None, None), P(), P(), P(), P())
    out_specs = P("sub", None, None, "tm")
    return jax.shard_map(
        on_device, mesh=mesh, in_specs=in_specs, out_specs=out_specs, check_vma=False
    )
```

profile of v0, /device:TPU:14, one launch (start us, length us, event | category | flops | bytes accessed | tf_op | source)
XLA Modules:
  0.0 792.8 jit_solution(15740473894358660357)
XLA Ops:
  1.4 5.8 copy.47
  7.1 5.2 gather_fusion
  12.4 2.1 fusion.51
  14.5 2.2 fusion.62
  16.7 2.8 copy.49
  20.6 1.3 copy.48
  23.4 5.5 copy.50
  28.9 5.2 reshape.129
  34.1 8.9 %convolution_convert_fusion = bf16[12,512,1024]{2,1,0:T(8,128)(2,1)} fusion(bf16[12,512,192]{2,1,0:T(8,128)(2,1)S(1)} %reshape.129, bf16[12,192,1024]{2,1,0:T(8,128)(2,1)} %bitcast.74), kind=kOutput, calls=%fused_computation.81 | convolution fusion | flops 2422210560 | bytes 19660800 | tf_op jit(solution)/shard_map/sqi,sit->sqt/dot_general | solution.py:78
  43.1 19.0 %reshape.131 = bf16[12,16,16,2,1024]{4,3,2,1,0:T(2,128)(2,1)} reshape(bf16[12,512,1024]{2,1,0:T(8,128)(2,1)} %convolution_convert_fusion) | data formatting | bytes 25165824 | tf_op jit(solution)/shard_map/reshape | solution.py:84
  62.1 12.5 %copy.52 = bf16[12,16,16,2,1024]{4,2,3,0,1:T(8,128)(2,1)} copy(bf16[12,16,16,2,1024]{4,3,2,1,0:T(2,128)(2,1)} %reshape.131) | data formatting | bytes 25165824 | tf_op jit(solution)/shard_map/reshape | solution.py:84
  74.6 6.2 all-to-all-start
  81.8 271.0 %all-to-all-done = bf16[12,16,16,2,1024]{4,2,3,0,1:T(8,128)(2,1)} async-done(((bf16[12,16,16,2,1024]{4,2,3,0,1:T(8,128)(2,1)}), bf16[12,16,16,2,1024]{4,2,3,0,1:T(8,128)(2,1)}, u32[]{:S(2)}, u32[]{:S(2)}) %all-to-all-start) | async-done | bytes 12582944 | tf_op jit(solution)/shard_map/all_to_all | solution.py:85
  352.8 12.8 %gather_fusion.1 = bf16[192,16,2,1024]{3,1,2,0:T(8,128)(2,1)} fusion(bf16[192,16,2,1024]{3,1,2,0:T(8,128)(2,1)} %bitcast.10, s32[1024]{0:T(1024)S(1)} %pad_clamp_fusion), kind=kCustom, calls=%fused_computation.1 | custom fusion | bytes 25166592 | tf_op jit(solution)/shard_map/jit(_take)/gather | solution.py:30
  365.6 6.8 select_bitcast_fusion
  372.4 12.4 %fusion.48 = f32[16,12,2,16,1024]{4,3,2,0,1:T(8,128)} fusion(bf16[12,16,16,2,1024,1]{4,2,3,1,0,5:T(8,128)(2,1)S(1)} %select_bitcast_fusion, bf16[1,16,2,16]{3,1,2,0:T(8,128)(2,1)S(1)} %get-tuple-element.26, bf16[1,16,2,16]{3,1,2,0:T(8,128)(2,1)S(1)} %get-tuple-element.25), kind=kOutput, calls=%fused_computation.80 | convolution fusion | flops 402657280 | bytes 37750784 | tf_op jit(solution)/shard_map/qkpc,gcbpt->bgqkt/dot_general | solution.py:36
  384.8 2.4 slice.415
  387.2 3.1 copy.54
  390.3 1.5 collective-permute-start
  391.8 35.0 %collective-permute-done = bf16[16,12,2,16,15]{3,0,4,2,1:T(8,128)(2,1)} collective-permute-done((bf16[16,12,2,16,15]{3,0,4,2,1:T(8,128)(2,1)S(1)}, bf16[16,12,2,16,15]{3,0,4,2,1:T(8,128)(2,1)}, u32[]{:S(2)}, u32[]{:S(2)}) %collective-permute-start) | collective-permute-done | bytes 184352 | tf_op jit(solution)/shard_map/ppermute | solution.py:12
  426.9 3.5 copy.55
  430.4 168.7 %fusion.47 = bf16[16,12,2,1024,16]{3,4,2,0,1:T(8,128)(2,1)} fusion(f32[16,12,2,16,1024]{4,3,2,0,1:T(8,128)} %fusion.48, f32[16,12,2,16,15]{4,3,2,0,1:T(8,128)S(1)} %copy.55, f32[16]{0:T(128)S(1)} %get-tuple-element.23, f32[16]{0:T(128)S(1)} %get-tuple-element.24, f32[16]{0:T(128)S(1)} %get-tuple-element.10, f32[16]{0:T(128)S(1)} %get-tuple-element.11, ...), kind=kLoop, calls=%fused_computation.79 | loop fusion | flops 295698432 | bytes 38118400 | tf_op jit(solution)/shard_map/convert_element_type | solution.py:56
  599.1 77.5 %copy.64 = bf16[16,12,2,1024,16]{4,3,2,1,0:T(8,128)(2,1)} copy(bf16[16,12,2,1024,16]{3,4,2,0,1:T(8,128)(2,1)} %fusion.47) | data formatting | bytes 25165824 | tf_op jit(solution)/shard_map/convert_element_type | solution.py:56
  676.7 116.1 %reshape.153 = bf16[16,12,2,16384]{3,2,1,0:T(2,128)(2,1)} reshape(bf16[16,12,2,1024,16]{4,3,2,1,0:T(8,128)(2,1)} %copy.64) | data formatting | bytes 25165824 | tf_op jit(solution)/shard_map/convert_element_type | solution.py:56
  (19 shorter events, 4.2 us)
Async XLA Ops:
  62.1 19.4 %copy-start.1 = (s32[192]{0:T(256)S(1)}, s32[192]{0:T(256)}, u32[]{:S(2)}) copy-start(s32[192]{0:T(256)} %param.9) | copy-start | bytes 2308
  74.6 278.2 %all-to-all-start = ((bf16[12,16,16,2,1024]{4,2,3,0,1:T(8,128)(2,1)}), bf16[12,16,16,2,1024]{4,2,3,0,1:T(8,128)(2,1)}, u32[]{:S(2)}, u32[]{:S(2)}) async-start(bf16[12,16,16,2,1024]{4,2,3,0,1:T(8,128)(2,1)} %copy.52), calls=%async_computation | async-start | bytes 25165824 | tf_op jit(solution)/shard_map/all_to_all | solution.py:85
  372.4 19.4 %copy-start = (f32[16,16]{1,0:T(8,128)S(1)}, f32[16,16]{1,0:T(8,128)}, u32[]{:S(2)}) copy-start(f32[16,16]{1,0:T(8,128)} %param.11) | copy-start | bytes 3076
  390.3 36.6 %collective-permute-start = (bf16[16,12,2,16,15]{3,0,4,2,1:T(8,128)(2,1)S(1)}, bf16[16,12,2,16,15]{3,0,4,2,1:T(8,128)(2,1)}, u32[]{:S(2)}, u32[]{:S(2)}) collective-permute-start(bf16[16,12,2,16,15]{3,0,4,2,1:T(8,128)(2,1)S(1)} %copy.54), channel_id=1, source_target_pairs={{0,1},{2,3},{4,5},{6,7},{8,9},{10,11},{12,13},{14,15},{16,17},{18,... | collective-permute-start | bytes 552968 | tf_op jit(solution)/shard_map/ppermute | solution.py:12
where the time goes:
time: 799 us; the launch traced here: 793 us
  waiting for transfers between devices  306 us (38%)
  local copies, waits for them, and re-layouts  275 us (34%)
  other arithmetic  182 us (23%)
  matrix products  21.3 us (3%)
    all_to_all x1, waiting for transfers between devices, on_device(): lax.all_to_all(blocks, 'sub', split_axis=1, concat_axis=0, tiled=True)[:, 0]  271 us
    convert_element_type x2, local copies, waits for them, and re-layouts, polyphase(): return jnp.swapaxes(running, 3, 4).reshape(channel_shape[0], channel_shap...  194 us
    convert_element_type x1, other arithmetic, polyphase(): return jnp.swapaxes(running, 3, 4).reshape(channel_shape[0], channel_shap...  169 us
    ppermute x1, waiting for transfers between devices, shifted(): return lax.ppermute(block, axis, route)  35 us
    reshape x2, local copies, waits for them, and re-layouts, on_device(): formed.reshape(local_subbands, axis_devices, beam_part, 2, local_time)  31.6 us
  transfers between devices with their start and end apart: 2, of which 2 were waited for; matrix products, arithmetic and copies ran while one was open for 0% of the time, Pallas kernels for 0%

commit v1 on v0

v1 whole, which is shorter than its diff:
```python
import functools
import math

import jax
import jax.numpy as jnp
from jax import lax
from jax.experimental import pallas as pl
from jax.experimental.pallas import tpu as pltpu
from jax.sharding import PartitionSpec as P

LANES = 128
VMEM = 60 * 1024 * 1024


def inverse_table(channel_count):
    channel_index = jnp.arange(channel_count, dtype=jnp.int32)
    phase = (jnp.outer(channel_index, channel_index) % channel_count).astype(jnp.float32) * (
        2.0 * math.pi / channel_count
    )
    cosine = jnp.cos(phase).astype(jnp.bfloat16)
    sine_table = jnp.sin(phase).astype(jnp.bfloat16)
    upper_rows = jnp.stack([cosine, -sine_table], axis=1)
    lower_rows = jnp.stack([sine_table, cosine], axis=1)
    return jnp.stack([upper_rows, lower_rows], axis=0)


def synthesis_matrix(filter_taps, inner, reach):
    tap_count, chan = filter_taps.shape
    table = inverse_table(chan).astype(jnp.float32)
    delta = jnp.arange(reach)[:, None, None]
    tl_in = jnp.arange(inner)[None, :, None]
    tl_out = jnp.arange(inner)[None, None, :]
    tap = inner * delta + tl_out - tl_in
    inside = (tap >= 0) & (tap < tap_count)
    taps = jnp.where(inside[..., None], filter_taps[jnp.clip(tap, 0, tap_count - 1)], 0.0)
    full = (
        taps[:, None, :, None, None, :, :]
        * table.transpose(2, 3, 0, 1)[None, :, None, :, :, None, :]
    )
    return full.reshape(reach * 2 * inner * chan, 2 * inner * chan).astype(jnp.bfloat16)


def form_kernel(inner, group, hot_ref, perm_ref, table_ref, volt_ref, rim_ref, *outs):
    chunks = outs[:-1]
    rim_out = outs[-1]
    f32, bf16 = jnp.float32, jnp.bfloat16
    real, imag = table_ref[0, 0], table_ref[0, 1]
    both = jnp.concatenate(
        [
            jnp.concatenate([real, -imag], axis=1),
            jnp.concatenate([imag, real], axis=1),
        ],
        axis=0,
    )
    weights = jnp.dot(hot_ref[...], both, preferred_element_type=f32).astype(bf16)
    rim_out[0] = jnp.dot(weights, rim_ref[0], preferred_element_type=f32).astype(bf16)
    signal = jnp.dot(volt_ref[0], perm_ref[...], preferred_element_type=f32).astype(bf16)
    rows = weights.shape[0] // len(chunks)
    for h, out in enumerate(chunks):
        formed = jnp.dot(
            weights[h * rows : (h + 1) * rows], signal, preferred_element_type=f32
        ).astype(bf16)
        for d in range(out.shape[0]):
            for tl in range(inner):
                out[d, 0, tl] = formed[
                    2 * d * group : 2 * (d + 1) * group, tl * LANES : (tl + 1) * LANES
                ]


def synth_kernel(inner, chan, group, reach, order_ref, live_ref, z_ref, rim_ref, mat_ref, *rest):
    out_ref, held, wide, line, stacked, made, sems = rest[-7:]
    g = pl.program_id(0)
    count = pl.num_programs(0)
    f32, bf16 = jnp.float32, jnp.bfloat16

    def fetch(step, slot):
        return [
            pltpu.make_async_copy(
                z_ref.at[order_ref[step * chan + c]], held.at[slot, c], sems.at[slot]
            )
            for c in range(chan)
        ]

    slot = lax.rem(g, 2)

    @pl.when(g == 0)
    def _():
        for copy in fetch(0, 0):
            copy.start()

    @pl.when(g + 1 < count)
    def _():
        for copy in fetch(g + 1, 1 - slot):
            copy.start()

    for copy in fetch(g, slot):
        copy.wait()

    pair = 2 * group
    for c in range(chan):
        alive = g * chan + c < live_ref[0]
        for tl in range(inner):
            block = held[slot, c, tl].astype(f32)
            wide[tl, c * pair : (c + 1) * pair, :] = jnp.where(alive, block, 0.0)

    width = inner * chan

    def turn(b, carry):
        base = pl.multiple_of(b * LANES, LANES)
        for p in range(2):
            rows = [
                wide[tl, pl.ds(p * group + b, chan, stride=pair), :] for tl in range(inner)
            ]
            line[p, 8 : 8 + LANES, :] = jnp.concatenate(rows, axis=0).T
            line[p, 8 - (reach - 1) : 8, :] = rim_ref[0, b, p]
            for delta in range(reach):
                at = (2 * delta + p) * width
                stacked[pl.ds(base, LANES), at : at + width] = line[
                    p, 8 - delta : 8 - delta + LANES, :
                ].astype(bf16)
        return carry

    lax.fori_loop(0, group, turn, 0, unroll=2)

    def emit(b, carry):
        base = pl.multiple_of(b * 2 * LANES, 2 * LANES)
        out = jnp.dot(
            stacked[pl.ds(base, 2 * LANES), :], mat_ref[...], preferred_element_type=f32
        )
        for i in range(2):
            for q in range(2):
                made[i, q * LANES : (q + 1) * LANES, :] = out[
                    i * LANES : (i + 1) * LANES, q * width : (q + 1) * width
                ]
        for i in range(2):
            for tb in range(LANES):
                both = made[i, pl.ds(tb, 2, stride=LANES), :].astype(bf16)
                out_ref[2 * b + i, 0, :, tb * LANES : (tb + 1) * LANES] = both
        return carry

    lax.fori_loop(0, group // 2, emit, 0)


def on_device(voltages, pointing_table, beam_pointing, subband_order, live_subbands, filter_taps):
    local_subbands, _, inputs, local_time = voltages.shape
    pointings = pointing_table.shape[2]
    beam_count = beam_pointing.shape[0]
    slots = subband_order.shape[0]
    tap_count, chan = filter_taps.shape
    inner = LANES // chan
    assert local_time == inner * LANES
    reach = 1 + -(-(tap_count - 1) // inner)
    rim_len = (reach - 1) * inner
    devices = lax.axis_size("sub")
    beam_part = beam_count // devices
    group = min(8, beam_part)
    chunk_count = beam_part // group
    bands = slots // chan

    signal = voltages.reshape(local_subbands, 2 * inputs, local_time)
    times = range(lax.axis_size("tm"))
    route = [(i - 1, i) for i in times if i > 0]
    rim = lax.ppermute(signal[:, :, local_time - rim_len :], "tm", route)
    rim = jnp.pad(rim, ((0, 0), (0, 0), (0, LANES - rim_len)))

    picks = beam_pointing.reshape(devices, chunk_count, 1, group).swapaxes(0, 1)
    wanted = (picks + pointings * jnp.arange(2)[:, None]).reshape(-1)
    hot = (wanted[:, None] == jnp.arange(2 * pointings)[None, :]).astype(jnp.bfloat16)
    source = jnp.arange(local_time, dtype=jnp.int32)
    place = (source % inner) * LANES + source // inner
    perm = (place[:, None] == source[None, :]).astype(jnp.bfloat16)

    piece = (devices, local_subbands, inner, 2 * group, LANES)
    made = pl.pallas_call(
        functools.partial(form_kernel, inner, group),
        grid=(local_subbands,),
        in_specs=[
            pl.BlockSpec(hot.shape, lambda s: (0, 0)),
            pl.BlockSpec(perm.shape, lambda s: (0, 0)),
            pl.BlockSpec((1, 2, pointings, inputs), lambda s: (s, 0, 0, 0)),
            pl.BlockSpec((1, 2 * inputs, local_time), lambda s: (s, 0, 0)),
            pl.BlockSpec((1, 2 * inputs, LANES), lambda s: (s, 0, 0)),
        ],
        out_specs=[
            pl.BlockSpec((devices, 1, inner, 2 * group, LANES), lambda s: (0, s, 0, 0, 0))
        ]
        * chunk_count
        + [pl.BlockSpec((1, 2 * beam_count, LANES), lambda s: (s, 0, 0))],
        out_shape=[jax.ShapeDtypeStruct(piece, jnp.bfloat16)] * chunk_count
        + [jax.ShapeDtypeStruct((local_subbands, 2 * beam_count, LANES), jnp.bfloat16)],
        compiler_params=pltpu.CompilerParams(vmem_limit_bytes=VMEM),
        cost_estimate=pl.CostEstimate(
            flops=12_000_000_000, bytes_accessed=20_000_000, transcendentals=0
        ),
        name="form",
    )(hot, perm, pointing_table, signal, rim)

    mat = synthesis_matrix(filter_taps, inner, reach)

    edge = made[-1][:, :, :rim_len].reshape(
        local_subbands, chunk_count, devices, 2 * group * rim_len
    )
    edge = edge.transpose(2, 0, 1, 3).reshape(devices, local_subbands, -1)
    edge = lax.all_to_all(edge, "sub", split_axis=0, concat_axis=0, tiled=True)
    edge = jnp.take(edge.reshape(slots, -1), subband_order, axis=0)
    live_mask = jnp.arange(slots, dtype=jnp.int32) < live_subbands[0]
    edge = jnp.where(live_mask[:, None], edge.astype(jnp.float32), 0.0)
    edge = edge.reshape(bands, chan, chunk_count, 2, group, reach - 1, inner)
    edge = edge.transpose(2, 0, 4, 3, 5, 6, 1).reshape(
        chunk_count, bands, group, 2, reach - 1, inner * chan
    )

    result = None
    for h in range(chunk_count):
        z = lax.all_to_all(made[h], "sub", split_axis=0, concat_axis=0, tiled=True)
        z = z.reshape(slots, inner, 2 * group, LANES)
        operands = [subband_order, live_subbands, z, edge[h], mat]
        in_specs = [
            pl.BlockSpec(memory_space=pl.ANY),
            pl.BlockSpec((1, group, 2, reach - 1, LANES), lambda g, *_: (g, 0, 0, 0, 0)),
            pl.BlockSpec(mat.shape, lambda g, *_: (0, 0)),
        ]
        alias = {}
        if result is not None:
            operands.append(result)
            in_specs.append(pl.BlockSpec(memory_space=pl.ANY))
            alias = {5: 0}
        result = pl.pallas_call(
            functools.partial(synth_kernel, inner, chan, group, reach),
            grid_spec=pltpu.PrefetchScalarGridSpec(
                num_scalar_prefetch=2,
                grid=(bands,),
                in_specs=in_specs,
                out_specs=pl.BlockSpec(
                    (group, 1, 2, local_time * chan), functools.partial(lambda h, g, *_: (h, g, 0, 0), h)
                ),
                scratch_shapes=[
                    pltpu.VMEM((2, chan, inner, 2 * group, LANES), jnp.bfloat16),
                    pltpu.VMEM((inner, chan * 2 * group, LANES), jnp.float32),
                    pltpu.VMEM((2, 8 + LANES, LANES), jnp.float32),
                    pltpu.VMEM((group * LANES, mat.shape[0]), jnp.bfloat16),
                    pltpu.VMEM((2, 2 * LANES, LANES), jnp.float32),
                    pltpu.SemaphoreType.DMA((2,)),
                ],
            ),
            out_shape=jax.ShapeDtypeStruct((beam_part, bands, 2, local_time * chan), jnp.bfloat16),
            input_output_aliases=alias,
            compiler_params=pltpu.CompilerParams(vmem_limit_bytes=VMEM),
            cost_estimate=pl.CostEstimate(
                flops=10_000_000_000, bytes_accessed=13_000_000, transcendentals=0
            ),
            name="synth",
        )(*operands)

    return result


def solution(mesh):
    in_specs = (P("sub", None, None, "tm"), P("sub", None, None, None), P(), P(), P(), P())
    out_specs = P("sub", None, None, "tm")
    return jax.shard_map(
        on_device, mesh=mesh, in_specs=in_specs, out_specs=out_specs, check_vma=False
    )
```

time: 799 us -> 375 us (0.47)
  local copies, waits for them, and re-layouts: 275 us -> 25.7 us
  waiting for transfers between devices: 306 us -> 83.6 us
  other arithmetic: 182 us -> 4.59 us
  blocking collectives: 0 us -> 158 us
  Pallas kernels: 0 us -> 92.9 us
  matrix products: 21.3 us -> 0 us
    convert_element_type x3 -> x1, local copies, waits for them, and re-layouts: 197 us -> 3.69 us  [synthesis_matrix(): full.reshape(reach * 2 * inner * chan, 2 * inner * chan)]
    all_to_all x1, waiting for transfers between devices: 271 us -> 83.6 us  [on_device(): z = lax.all_to_all(made[h], 'sub', split_axis=0, concat_axis=0, tiled=True)]
    convert_element_type x1 -> x3, other arithmetic: 169 us -> 3.55 us  [the longest x1 1.75 us: on_device(): perm = (place[:, None] == source[None, :]).astype(jnp.bfloat16)]
    all_to_all x0 -> x2, blocking collectives: none -> 158 us  [the longest x1 144 us: on_device(): z = lax.all_to_all(made[h], 'sub', split_axis=0, concat_axis=0, tiled=True)]
    pallas_call x0 -> x3, Pallas kernels: none -> 92.9 us  [the longest x2 69 us: on_device(): pl.pallas_call(functools.partial(synth_kernel, inner, chan, group, reach)...]
    ppermute x1, waiting for transfers between devices: 35 us -> 0.01 us  [on_device(): rim = lax.ppermute(signal[:, :, local_time - rim_len:], 'tm', route)]
    reshape x3 -> x5, local copies, waits for them, and re-layouts: 36.8 us -> 3.72 us  [the longest x1 2.61 us: on_device(): made[-1][:, :, :rim_len]]
    dot_general x2 -> x0, matrix products: 21.3 us -> none  [the longest x1 12.4 us: spectrum_channels(): jnp.einsum('qkpc,gcbpt->bgqkt', inverse_rows, grouped, preferred_element_...]
  transfers between devices with their start and end apart: 2 -> 2, of which waited for: 2 -> 1; matrix products, arithmetic and copies ran while one was open for 0% -> 7% of each run, Pallas kernels for 0% -> 9%
where the time goes in v1:
time: 375 us; the launch traced here: 372 us
  blocking collectives  158 us (42%)
  Pallas kernels  92.9 us (25%)
  waiting for transfers between devices  83.6 us (22%)
  local copies, waits for them, and re-layouts  25.7 us (7%)
  starting transfers between devices  6.66 us (2%)
  other arithmetic  4.59 us (1%)
    all_to_all x1, blocking collectives, on_device(): z = lax.all_to_all(made[h], 'sub', split_axis=0, concat_axis=0, tiled=True)  144 us
    all_to_all x1, waiting for transfers between devices, on_device(): z = lax.all_to_all(made[h], 'sub', split_axis=0, concat_axis=0, tiled=True)  83.6 us
    pallas_call x2, Pallas kernels, on_device(): pl.pallas_call(functools.partial(synth_kernel, inner, chan, group, reach)...  69 us
    pallas_call x1, Pallas kernels, on_device(): pl.pallas_call(functools.partial(form_kernel, inner, group), grid=(local_...  23.9 us
    all_to_all x1, blocking collectives, on_device(): edge = lax.all_to_all(edge, 'sub', split_axis=0, concat_axis=0, tiled=True)  13.7 us
  transfers between devices with their start and end apart: 2, of which 1 were waited for; matrix products, arithmetic and copies ran while one was open for 7% of the time, Pallas kernels for 9%

profile of v1, /device:TPU:14, one launch (start us, length us, event | category | flops | bytes accessed | tf_op | source)
XLA Modules:
  0.0 372.1 jit_solution(9477697211266962896)
XLA Ops:
  0.0 1.4 slice.22
  1.7 1.3 collective-permute-start
  3.0 0.8 reshape.228
  4.0 1.8 fusion.perm_ref
  5.7 1.0 fusion.1.hot_ref
  6.8 2.4 copy.23.table_ref
  9.5 1.0 pad.4.rim_ref
  10.4 23.9 %form.1 = (bf16[16,12,8,16,128]{4,3,2,1,0:T(8,128)(2,1)}, bf16[16,12,8,16,128]{4,3,2,1,0:T(8,128)(2,1)}, bf16[12,512,128]{2,1,0:T(8,128)(2,1)}) custom-call(bf16[512,640]{1,0:T(8,128)(2,1)} %fusion.1.hot_ref, bf16[1024,1024]{1,0:T(8,128)(2,1)} %fusion.perm_ref, bf16[12,2,320,96]{3,2,1,0:T(8,128)(2,1)} %copy.23.table_ref, bf16[12,192,1024]{2,1,0:T(8,128)(2,1)} %bitcast.36, ...), custom_call_target="tpu_custom_call" | custom-call | flops 12000000000 | bytes 20000000 | tf_op jit(solution)/shard_map/form/pallas_call | solution.py:174
  34.4 2.6 reshape.231
  37.3 13.7 %all_to_all.15 = bf16[16,12,512]{2,1,0:T(8,128)(2,1)S(1)} all-to-all(bf16[16,12,512]{2,1,0:T(8,128)(2,1)S(1)} %reshape.253), channel_id=1, replica_groups=mesh['sub'=16,'tm'=2] {'sub'}, dimensions={0} | all-to-all | bytes 393216 | tf_op jit(solution)/shard_map/all_to_all | solution.py:204
  51.0 143.9 %all_to_all.16 = bf16[16,12,8,16,128]{4,3,2,1,0:T(8,128)(2,1)} all-to-all(bf16[16,12,8,16,128]{4,3,2,1,0:T(8,128)(2,1)} %get-tuple-element.10), channel_id=1, replica_groups=mesh['sub'=16,'tm'=2] {'sub'}, dimensions={0} | all-to-all | bytes 12582912 | tf_op jit(solution)/shard_map/all_to_all | solution.py:215
  194.8 5.4 %all-to-all-start = ((bf16[16,12,8,16,128]{4,3,2,1,0:T(8,128)(2,1)}), bf16[16,12,8,16,128]{4,3,2,1,0:T(8,128)(2,1)}, u32[]{:S(2)}, u32[]{:S(2)}) async-start(bf16[16,12,8,16,128]{4,3,2,1,0:T(8,128)(2,1)} %get-tuple-element.8), calls=%async_computation | async-start | bytes 12582912 | tf_op jit(solution)/shard_map/all_to_all | solution.py:215
  201.4 0.7 gather_fusion.1
  202.2 0.8 multiply_convert_fusion
  203.0 3.7 convert_element_type.77.mat_ref
  206.8 1.0 gather_fusion
  207.9 1.4 gather.10
  210.5 1.6 copy.29
  212.1 2.8 squeeze.11.rim_ref
  214.9 1.6 copy.27
  216.5 2.8 squeeze.10.rim_ref
  219.3 34.4 %synth.2.rest_0_ = bf16[16,12,2,16384]{3,2,1,0:T(2,128)(2,1)} custom-call(s32[192]{0:T(256)} %order_ref.3, s32[1]{0:T(128)} %copy.33.live_ref, bf16[192,8,16,128]{3,2,1,0:T(8,128)(2,1)} %bitcast.31, f32[12,8,2,2,128]{4,3,2,1,0:T(2,128)} %squeeze.11.rim_ref, bf16[768,256]{1,0:T(8,128)(2,1)} %convert_element_type.77.mat_ref), custom_call_target="tpu_custom_call" | custom-call | flops 10000000000 | bytes 13000000 | tf_op jit(solution)/shard_map/synth/pallas_call | solution.py:228
  253.7 83.6 %all-to-all-done = bf16[16,12,8,16,128]{4,3,2,1,0:T(8,128)(2,1)} async-done(((bf16[16,12,8,16,128]{4,3,2,1,0:T(8,128)(2,1)}), bf16[16,12,8,16,128]{4,3,2,1,0:T(8,128)(2,1)}, u32[]{:S(2)}, u32[]{:S(2)}) %all-to-all-start) | async-done | bytes 6291488 | tf_op jit(solution)/shard_map/all_to_all | solution.py:215
  337.4 34.6 %synth.3 = bf16[16,12,2,16384]{3,2,1,0:T(2,128)(2,1)} custom-call(s32[192]{0:T(256)} %order_ref.3, s32[1]{0:T(128)} %copy.33.live_ref, bf16[192,8,16,128]{3,2,1,0:T(8,128)(2,1)} %bitcast.3.z_ref, f32[12,8,2,2,128]{4,3,2,1,0:T(2,128)} %squeeze.10.rim_ref, bf16[768,256]{1,0:T(8,128)(2,1)} %convert_element_type.77.mat_ref, ...), custom_call_target="tpu_custom_call", output_to_operand_aliasing={{}: (5, {})} | custom-call | flops 10000000000 | bytes 13000000 | tf_op jit(solution)/shard_map/synth/pallas_call | solution.py:228
  (39 shorter events, 2.9 us)
Async XLA Ops:
  0.0 201.4 %copy-start = (f32[16,16]{1,0:T(8,128)S(1)}, f32[16,16]{1,0:T(8,128)}, u32[]{:S(2)}) copy-start(f32[16,16]{1,0:T(8,128)} %param.11) | copy-start | bytes 3076
  0.0 6.8 %copy-start.2 = (bf16[12,2,320,96]{2,3,1,0:T(8,128)(2,1)S(1)}, bf16[12,2,320,96]{2,3,1,0:T(8,128)(2,1)}, u32[]{:S(2)}) copy-start(bf16[12,2,320,96]{2,3,1,0:T(8,128)(2,1)} %param.7) | copy-start | bytes 4423684
  1.7 7.5 %collective-permute-start = (bf16[12,192,16]{1,2,0:T(8,128)(2,1)S(1)}, bf16[12,192,16]{1,2,0:T(8,128)(2,1)S(1)}, u32[]{:S(2)}, u32[]{:S(2)}) collective-permute-start(bf16[12,192,16]{1,2,0:T(8,128)(2,1)S(1)} %copy.21), channel_id=1, source_target_pairs={{0,1},{2,3},{4,5},{6,7},{8,9},{10,11},{12,13},{14,15},{16,17},{18,... | collective-permute-start | bytes 221192 | tf_op jit(solution)/shard_map/ppermute | solution.py:163
  194.8 6.0 %copy-start.3 = (s32[192]{0:T(256)S(1)}, s32[192]{0:T(256)}, u32[]{:S(2)}) copy-start(s32[192]{0:T(256)} %order_ref.3) | copy-start | bytes 2308
  194.8 142.5 %all-to-all-start = ((bf16[16,12,8,16,128]{4,3,2,1,0:T(8,128)(2,1)}), bf16[16,12,8,16,128]{4,3,2,1,0:T(8,128)(2,1)}, u32[]{:S(2)}, u32[]{:S(2)}) async-start(bf16[16,12,8,16,128]{4,3,2,1,0:T(8,128)(2,1)} %get-tuple-element.8), calls=%async_computation | async-start | bytes 12582912 | tf_op jit(solution)/shard_map/all_to_all | solution.py:215
  337.3 34.6 %copy-start.1 = (f32[16,16]{1,0:T(8,128)S(1)}, f32[16,16]{1,0:T(8,128)}, u32[]{:S(2)}) copy-start(f32[16,16]{1,0:T(8,128)} %param.11) | copy-start | bytes 3076

commit v2 on v1

--- a/solution.py
+++ b/solution.py
@@ -40,9 +40,8 @@
     return full.reshape(reach * 2 * inner * chan, 2 * inner * chan).astype(jnp.bfloat16)
 
 
-def form_kernel(inner, group, hot_ref, perm_ref, table_ref, volt_ref, rim_ref, *outs):
-    chunks = outs[:-1]
-    rim_out = outs[-1]
+def form_kernel(inner, groups, with_rim, hot_ref, perm_ref, table_ref, volt_ref, *rest):
+    chunks = rest[-len(groups) :]
     f32, bf16 = jnp.float32, jnp.bfloat16
     real, imag = table_ref[0, 0], table_ref[0, 1]
     both = jnp.concatenate(
@@ -53,13 +52,17 @@
         axis=0,
     )
     weights = jnp.dot(hot_ref[...], both, preferred_element_type=f32).astype(bf16)
-    rim_out[0] = jnp.dot(weights, rim_ref[0], preferred_element_type=f32).astype(bf16)
+    if with_rim:
+        rim_ref, rim_out = rest[0], rest[1]
+        rim_out[0] = jnp.dot(weights, rim_ref[0], preferred_element_type=f32).astype(bf16)
     signal = jnp.dot(volt_ref[0], perm_ref[...], preferred_element_type=f32).astype(bf16)
-    rows = weights.shape[0] // len(chunks)
-    for h, out in enumerate(chunks):
+    start = 0 if with_rim else hot_ref.shape[0] - 2 * sum(groups) * chunks[0].shape[0]
+    for group, out in zip(groups, chunks):
+        rows = 2 * group * out.shape[0]
         formed = jnp.dot(
-            weights[h * rows : (h + 1) * rows], signal, preferred_element_type=f32
+            weights[start : start + rows], signal, preferred_element_type=f32
         ).astype(bf16)
+        start += rows
         for d in range(out.shape[0]):
             for tl in range(inner):
                 out[d, 0, tl] = formed[
@@ -67,18 +70,23 @@
                 ]
 
 
-def synth_kernel(inner, chan, group, reach, order_ref, live_ref, z_ref, rim_ref, mat_ref, *rest):
+def synth_kernel(
+    inner, chan, group, reach, local, order_ref, live_ref, z_ref, rim_ref, mat_ref, *rest
+):
     out_ref, held, wide, line, stacked, made, sems = rest[-7:]
     g = pl.program_id(0)
     count = pl.num_programs(0)
     f32, bf16 = jnp.float32, jnp.bfloat16
 
     def fetch(step, slot):
+        named = [order_ref[step * chan + c] for c in range(chan)]
         return [
             pltpu.make_async_copy(
-                z_ref.at[order_ref[step * chan + c]], held.at[slot, c], sems.at[slot]
+                z_ref.at[lax.div(at, local), pl.ds(lax.rem(at, local) * inner, inner)],
+                held.at[slot, c],
+                sems.at[slot],
             )
-            for c in range(chan)
+            for c, at in enumerate(named)
         ]
 
     slot = lax.rem(g, 2)
@@ -153,8 +161,12 @@
     rim_len = (reach - 1) * inner
     devices = lax.axis_size("sub")
     beam_part = beam_count // devices
-    group = min(8, beam_part)
-    chunk_count = beam_part // group
+    quarter = beam_part // 4
+    if beam_part % 8 == 0:
+        groups, firsts = [quarter, 2 * quarter, quarter], [0, 2 * quarter, quarter]
+    else:
+        groups, firsts = [beam_part], [0]
+    starts = [sum(groups[:h]) for h in range(len(groups))]
     bands = slots // chan
 
     signal = voltages.reshape(local_subbands, 2 * inputs, local_time)
@@ -163,58 +175,93 @@
     rim = lax.ppermute(signal[:, :, local_time - rim_len :], "tm", route)
     rim = jnp.pad(rim, ((0, 0), (0, 0), (0, LANES - rim_len)))
 
-    picks = beam_pointing.reshape(devices, chunk_count, 1, group).swapaxes(0, 1)
-    wanted = (picks + pointings * jnp.arange(2)[:, None]).reshape(-1)
+    picks = beam_pointing.reshape(devices, beam_part)
+    wanted = jnp.concatenate(
+        [
+            (
+                picks[:, None, first : first + group]
+                + pointings * jnp.arange(2, dtype=jnp.int32)[:, None]
+            ).reshape(-1)
+            for first, group in zip(firsts, groups)
+        ]
+    )
     hot = (wanted[:, None] == jnp.arange(2 * pointings)[None, :]).astype(jnp.bfloat16)
     source = jnp.arange(local_time, dtype=jnp.int32)
     place = (source % inner) * LANES + source // inner
     perm = (place[:, None] == source[None, :]).astype(jnp.bfloat16)
 
-    piece = (devices, local_subbands, inner, 2 * group, LANES)
-    made = pl.pallas_call(
-        functools.partial(form_kernel, inner, group),
-        grid=(local_subbands,),
-        in_specs=[
-            pl.BlockSpec(hot.shape, lambda s: (0, 0)),
-            pl.BlockSpec(perm.shape, lambda s: (0, 0)),
-            pl.BlockSpec((1, 2, pointings, inputs), lambda s: (s, 0, 0, 0)),
-            pl.BlockSpec((1, 2 * inputs, local_time), lambda s: (s, 0, 0)),
-            pl.BlockSpec((1, 2 * inputs, LANES), lambda s: (s, 0, 0)),
+    def form(groups, signal, rim):
+        with_rim = rim is not None
+        pieces = [(devices, local_subbands, inner, 2 * group, LANES) for group in groups]
+        rim_size = (local_subbands, hot.shape[0], LANES)
+        return pl.pallas_call(
+            functools.partial(form_kernel, inner, groups, with_rim),
+            grid=(local_subbands,),
+            in_specs=[
+                pl.BlockSpec(hot.shape, lambda s: (0, 0)),
+                pl.BlockSpec(perm.shape, lambda s: (0, 0)),
+                pl.BlockSpec((1, 2, pointings, inputs), lambda s: (s, 0, 0, 0)),
+                pl.BlockSpec((1, 2 * inputs, local_time), lambda s: (s, 0, 0)),
+            ]
+            + [pl.BlockSpec((1, 2 * inputs, LANES), lambda s: (s, 0, 0))] * with_rim,
+            out_specs=[pl.BlockSpec((1,) + rim_size[1:], lambda s: (s, 0, 0))] * with_rim
+            + [
+                pl.BlockSpec((size[0], 1) + size[2:], lambda s: (0, s, 0, 0, 0))
+                for size in pieces
+            ],
+            out_shape=[jax.ShapeDtypeStruct(rim_size, jnp.bfloat16)] * with_rim
+            + [jax.ShapeDtypeStruct(size, jnp.bfloat16) for size in pieces],
+            compiler_params=pltpu.CompilerParams(vmem_limit_bytes=VMEM),
+            cost_estimate=pl.CostEstimate(
+                flops=12_000_000_000, bytes_accessed=20_000_000, transcendentals=0
+            ),
+            name="form",
+        )(hot, perm, pointing_table, signal, *([rim] if with_rim else []))
+
+    edge, opening = form(groups[:1], signal, rim)
+    pieces = [opening]
+    if len(groups) > 1:
+        later, _ = lax.optimization_barrier((signal, opening))
+        pieces += form(groups[1:], later, None)
+
+    mat = synthesis_matrix(filter_taps, inner, reach)
+
+    edge = edge[:, :, :rim_len]
+    edge = jnp.concatenate(
+        [
+            edge[:, 2 * devices * start : 2 * devices * (start + group)].reshape(
+                local_subbands, devices, 2 * group * rim_len
+            )
+            for start, group in zip(starts, groups)
         ],
-        out_specs=[
-            pl.BlockSpec((devices, 1, inner, 2 * group, LANES), lambda s: (0, s, 0, 0, 0))
-        ]
-        * chunk_count
-        + [pl.BlockSpec((1, 2 * beam_count, LANES), lambda s: (s, 0, 0))],
-        out_shape=[jax.ShapeDtypeStruct(piece, jnp.bfloat16)] * chunk_count
-        + [jax.ShapeDtypeStruct((local_subbands, 2 * beam_count, LANES), jnp.bfloat16)],
-        compiler_params=pltpu.CompilerParams(vmem_limit_bytes=VMEM),
-        cost_estimate=pl.CostEstimate(
-            flops=12_000_000_000, bytes_accessed=20_000_000, transcendentals=0
-        ),
-        name="form",
-    )(hot, perm, pointing_table, signal, rim)
-
-    mat = synthesis_matrix(filter_taps, inner, reach)
-
-    edge = made[-1][:, :, :rim_len].reshape(
-        local_subbands, chunk_count, devices, 2 * group * rim_len
-    )
-    edge = edge.transpose(2, 0, 1, 3).reshape(devices, local_subbands, -1)
-    edge = lax.all_to_all(edge, "sub", split_axis=0, concat_axis=0, tiled=True)
+        axis=2,
+    )
+    edge = edge.swapaxes(0, 1).reshape(devices, -1)
+    edge_size = edge.shape[1]
+    planes = -(-edge_size // (2 * groups[0] * LANES))
+    edge = jnp.pad(edge, ((0, 0), (0, planes * 2 * groups[0] * LANES - edge_size)))
+    edge = edge.reshape(devices, planes, 2 * groups[0], LANES)
+    pieces = [
+        piece.reshape(devices, local_subbands * inner, 2 * group, LANES)
+        for piece, group in zip(pieces, groups)
+    ]
+    pieces[0] = jnp.concatenate([pieces[0], edge], axis=1)
+    got = [lax.all_to_all(p, "sub", split_axis=0, concat_axis=0, tiled=True) for p in pieces]
+    edge = got[0][:, local_subbands * inner :].reshape(devices, -1)[:, :edge_size]
     edge = jnp.take(edge.reshape(slots, -1), subband_order, axis=0)
     live_mask = jnp.arange(slots, dtype=jnp.int32) < live_subbands[0]
     edge = jnp.where(live_mask[:, None], edge.astype(jnp.float32), 0.0)
-    edge = edge.reshape(bands, chan, chunk_count, 2, group, reach - 1, inner)
-    edge = edge.transpose(2, 0, 4, 3, 5, 6, 1).reshape(
-        chunk_count, bands, group, 2, reach - 1, inner * chan
-    )
+
+    def edge_of(start, group):
+        part = edge[:, 2 * start * rim_len : 2 * (start + group) * rim_len]
+        part = part.reshape(bands, chan, 2, group, reach - 1, inner)
+        return part.transpose(0, 3, 2, 4, 5, 1).reshape(
+            bands, group, 2, reach - 1, inner * chan
+        )
 
     result = None
-    for h in range(chunk_count):
-        z = lax.all_to_all(made[h], "sub", split_axis=0, concat_axis=0, tiled=True)
-        z = z.reshape(slots, inner, 2 * group, LANES)
-        operands = [subband_order, live_subbands, z, edge[h], mat]
+    for first, start, group, z in zip(firsts, starts, groups, got):
+        operands = [subband_order, live_subbands, z, edge_of(start, group), mat]
         in_specs = [
             pl.BlockSpec(memory_space=pl.ANY),
             pl.BlockSpec((1, group, 2, reach - 1, LANES), lambda g, *_: (g, 0, 0, 0, 0)),
@@ -226,13 +273,13 @@
             in_specs.append(pl.BlockSpec(memory_space=pl.ANY))
             alias = {5: 0}
         result = pl.pallas_call(
-            functools.partial(synth_kernel, inner, chan, group, reach),
+            functools.partial(synth_kernel, inner, chan, group, reach, local_subbands),
             grid_spec=pltpu.PrefetchScalarGridSpec(
                 num_scalar_prefetch=2,
                 grid=(bands,),
                 in_specs=in_specs,
                 out_specs=pl.BlockSpec(
-                    (group, 1, 2, local_time * chan), functools.partial(lambda h, g, *_: (h, g, 0, 0), h)
+                    (group, 1, 2, local_time * chan), functools.partial(lambda h, g, *_: (h, g, 0, 0), first // group)
                 ),
                 scratch_shapes=[
                     pltpu.VMEM((2, chan, inner, 2 * group, LANES), jnp.bfloat16),

time: 375 us -> 369 us (0.984)
  waiting for transfers between devices: 83.6 us -> 56.3 us
  Pallas kernels: 92.9 us -> 113 us
  blocking collectives: 158 us -> 142 us
  starting transfers between devices: 6.66 us -> 13.2 us
  local copies, waits for them, and re-layouts: 25.7 us -> 30.9 us
    all_to_all x1 -> x2, waiting for transfers between devices: 83.6 us -> 56.3 us  [on_device(): lax.all_to_all(p, 'sub', split_axis=0, concat_axis=0, tiled=True)]
    pallas_call x3 -> x5, Pallas kernels: 92.9 us -> 113 us  [the longest x3 74.3 us: on_device(): pl.pallas_call(functools.partial(synth_kernel, inner, chan, group, reach,...]
    all_to_all x2 -> x1, blocking collectives: 158 us -> 142 us  [on_device(): lax.all_to_all(p, 'sub', split_axis=0, concat_axis=0, tiled=True)]
    reshape x5 -> x11, local copies, waits for them, and re-layouts: 3.72 us -> 12.7 us  [the longest x3 5.23 us: on_device(): edge[:, 2 * devices * start:2 * devices * (start + group)]]
    all_to_all x1 -> x2, starting transfers between devices: 5.37 us -> 11.9 us  [on_device(): lax.all_to_all(p, 'sub', split_axis=0, concat_axis=0, tiled=True)]
    squeeze x2 -> x0, local copies, waits for them, and re-layouts: 5.54 us -> none  [on_device(): operands = [subband_order, live_subbands, z, edge[h], mat]]
  transfers between devices with their start and end apart: 2 -> 3, of which waited for: 1 -> 1; matrix products, arithmetic and copies ran while one was open for 7% -> 6% of each run, Pallas kernels for 9% -> 20%
where the time goes in v2:
time: 369 us; the launch traced here: 365 us
  blocking collectives  142 us (38%)
  Pallas kernels  113 us (31%)
  waiting for transfers between devices  56.3 us (15%)
  local copies, waits for them, and re-layouts  30.9 us (8%)
  starting transfers between devices  13.2 us (4%)
  other arithmetic  8.07 us (2%)
    all_to_all x1, blocking collectives, on_device(): lax.all_to_all(p, 'sub', split_axis=0, concat_axis=0, tiled=True)  142 us
    pallas_call x3, Pallas kernels, on_device(): pl.pallas_call(functools.partial(synth_kernel, inner, chan, group, reach,...  74.3 us
    all_to_all x2, waiting for transfers between devices, on_device(): lax.all_to_all(p, 'sub', split_axis=0, concat_axis=0, tiled=True)  56.3 us
    pallas_call x2, Pallas kernels, form(): pl.pallas_call(functools.partial(form_kernel, inner, groups, with_rim), g...  39 us
    all_to_all x2, starting transfers between devices, on_device(): lax.all_to_all(p, 'sub', split_axis=0, concat_axis=0, tiled=True)  11.9 us
  transfers between devices with their start and end apart: 3, of which 1 were waited for; matrix products, arithmetic and copies ran while one was open for 6% of the time, Pallas kernels for 20%

profile of v2, /device:TPU:14, one launch (start us, length us, event | category | flops | bytes accessed | tf_op | source)
XLA Modules:
  0.0 364.9 jit_solution(16210590570302864058)
XLA Ops:
  0.0 1.4 slice.55
  1.7 1.3 collective-permute-start
  4.4 1.8 fusion.perm_ref
  6.2 1.0 fusion.1.hot_ref
  7.2 2.4 copy.31.table_ref
  10.8 21.4 %form.2 = (bf16[12,512,128]{2,1,0:T(8,128)(2,1)}, bf16[16,12,8,8,128]{4,3,2,1,0:T(8,128)(2,1)}) custom-call(bf16[512,640]{1,0:T(8,128)(2,1)} %fusion.1.hot_ref, bf16[1024,1024]{1,0:T(8,128)(2,1)} %fusion.perm_ref, bf16[12,2,320,96]{3,2,1,0:T(8,128)(2,1)} %copy.31.table_ref, bf16[12,192,1024]{2,1,0:T(8,128)(2,1)} %bitcast.46, bf16[12,192,128]{2,1,0:T(8,128)(2,1)} %pad.4.rest_0_), custom_call_target="tpu_custom_call" | custom-call | flops 12000000000 | bytes 20000000 | tf_op jit(solution)/shard_map/form/pallas_call | solution.py:197
  32.2 2.2 slice.42
  34.5 1.9 fusion.21
  36.4 2.4 reshape.244
  38.8 1.9 reshape.243
  43.5 2.9 pad_maximum_fusion
  46.4 6.2 %all-to-all-start.1 = ((bf16[16,102,8,128]{3,2,1,0:T(8,128)(2,1)}), bf16[16,102,8,128]{3,2,1,0:T(8,128)(2,1)S(1)}, u32[]{:S(2)}, u32[]{:S(2)}) async-start(bf16[16,102,8,128]{3,2,1,0:T(8,128)(2,1)} %pad_maximum_fusion), calls=%async_computation.1 | async-start | bytes 6684672 | tf_op jit(solution)/shard_map/all_to_all | solution.py:249
  52.7 17.6 %form.3 = (bf16[16,12,8,16,128]{4,3,2,1,0:T(8,128)(2,1)}, bf16[16,12,8,8,128]{4,3,2,1,0:T(8,128)(2,1)}) custom-call(bf16[512,640]{1,0:T(8,128)(2,1)} %fusion.1.hot_ref, bf16[1024,1024]{1,0:T(8,128)(2,1)} %fusion.perm_ref, bf16[12,2,320,96]{3,2,1,0:T(8,128)(2,1)} %copy.31.table_ref, bf16[12,192,1024]{2,1,0:T(8,128)(2,1)} %bitcast.47), custom_call_target="tpu_custom_call" | custom-call | flops 12000000000 | bytes 20000000 | tf_op jit(solution)/shard_map/form/pallas_call | solution.py:197
  70.2 56.3 %all-to-all-done.1.z_ref = bf16[16,102,8,128]{3,2,1,0:T(8,128)(2,1)S(1)} async-done(((bf16[16,102,8,128]{3,2,1,0:T(8,128)(2,1)}), bf16[16,102,8,128]{3,2,1,0:T(8,128)(2,1)S(1)}, u32[]{:S(2)}, u32[]{:S(2)}) %all-to-all-start.1) | async-done | bytes 3342368 | tf_op jit(solution)/shard_map/all_to_all | solution.py:249
  126.5 142.0 %all_to_all.15.z_ref = bf16[16,96,16,128]{3,2,1,0:T(8,128)(2,1)} all-to-all(bf16[16,96,16,128]{3,2,1,0:T(8,128)(2,1)} %bitcast.39), channel_id=1, replica_groups=mesh['sub'=16,'tm'=2] {'sub'}, dimensions={0} | all-to-all | bytes 12582912 | tf_op jit(solution)/shard_map/all_to_all | solution.py:249
  268.5 5.7 %all-to-all-start = ((bf16[16,96,8,128]{3,2,1,0:T(8,128)(2,1)}), bf16[16,96,8,128]{3,2,1,0:T(8,128)(2,1)}, u32[]{:S(2)}, u32[]{:S(2)}) async-start(bf16[16,96,8,128]{3,2,1,0:T(8,128)(2,1)} %bitcast.42), calls=%async_computation | async-start | bytes 6291456 | tf_op jit(solution)/shard_map/all_to_all | solution.py:249
  276.9 3.7 %convert_element_type.78.mat_ref = bf16[768,256]{1,0:T(8,128)(2,1)} reshape(bf16[3,2,8,16,2,8,16]{6,5,4,3,2,1,0:T(8,128)(2,1)S(1)} %multiply_convert_fusion) | data formatting | bytes 786432 | tf_op jit(solution)/shard_map/convert_element_type | solution.py:40
  280.8 1.0 gather_fusion
  282.9 1.0 reshape.248.rim_ref
  286.0 1.6 copy.37
  287.7 2.7 reshape.251.rim_ref
  290.4 19.7 %synth.3.rest_0_ = bf16[16,12,2,16384]{3,2,1,0:T(2,128)(2,1)} custom-call(s32[192]{0:T(256)} %order_ref.5, s32[1]{0:T(128)} %copy.42.live_ref, bf16[16,102,8,128]{3,2,1,0:T(8,128)(2,1)} %copy-done.2, f32[12,4,2,2,128]{4,3,2,1,0:T(2,128)} %reshape.253.rim_ref, bf16[768,256]{1,0:T(8,128)(2,1)} %convert_element_type.78.mat_ref), custom_call_target="tpu_custom_call" | custom-call | flops 10000000000 | bytes 13000000 | tf_op jit(solution)/shard_map/synth/pallas_call | solution.py:275
  310.1 34.8 %synth.4.rest_0_ = bf16[16,12,2,16384]{3,2,1,0:T(2,128)(2,1)} custom-call(s32[192]{0:T(256)} %order_ref.5, s32[1]{0:T(128)} %copy.42.live_ref, bf16[16,96,16,128]{3,2,1,0:T(8,128)(2,1)} %all_to_all.15.z_ref, f32[12,8,2,2,128]{4,3,2,1,0:T(2,128)} %reshape.251.rim_ref, bf16[768,256]{1,0:T(8,128)(2,1)} %convert_element_type.78.mat_ref, ...), custom_call_target="tpu_custom_call", output_to_operand_aliasing={{}: (5, {})} | custom-call | flops 10000000000 | bytes 13000000 | tf_op jit(solution)/shard_map/synth/pallas_call | solution.py:275
  344.9 19.8 %synth.5 = bf16[16,12,2,16384]{3,2,1,0:T(2,128)(2,1)} custom-call(s32[192]{0:T(256)} %order_ref.5, s32[1]{0:T(128)} %copy.42.live_ref, bf16[16,96,8,128]{3,2,1,0:T(8,128)(2,1)} %all-to-all-done.z_ref, f32[12,4,2,2,128]{4,3,2,1,0:T(2,128)} %reshape.248.rim_ref, bf16[768,256]{1,0:T(8,128)(2,1)} %convert_element_type.78.mat_ref, ...), custom_call_target="tpu_custom_call", output_to_operand_aliasing={{}: (5, {})} | custom-call | flops 10000000000 | bytes 13000000 | tf_op jit(solution)/shard_map/synth/pallas_call | solution.py:275
  (64 shorter events, 11.0 us)
Async XLA Ops:
  0.0 275.3 %copy-start = (f32[16,16]{1,0:T(8,128)S(1)}, f32[16,16]{1,0:T(8,128)}, u32[]{:S(2)}) copy-start(f32[16,16]{1,0:T(8,128)} %param.11) | copy-start | bytes 3076
  0.0 7.2 %copy-start.4 = (bf16[12,2,320,96]{2,3,1,0:T(8,128)(2,1)S(1)}, bf16[12,2,320,96]{2,3,1,0:T(8,128)(2,1)}, u32[]{:S(2)}) copy-start(bf16[12,2,320,96]{2,3,1,0:T(8,128)(2,1)} %param.7) | copy-start | bytes 4423684
  1.7 7.9 %collective-permute-start = (bf16[12,192,16]{1,2,0:T(8,128)(2,1)S(1)}, bf16[12,192,16]{1,2,0:T(8,128)(2,1)S(1)}, u32[]{:S(2)}, u32[]{:S(2)}) collective-permute-start(bf16[12,192,16]{1,2,0:T(8,128)(2,1)S(1)} %copy.28), channel_id=1, source_target_pairs={{0,1},{2,3},{4,5},{6,7},{8,9},{10,11},{12,13},{14,15},{16,17},{18,... | collective-permute-start | bytes 221192 | tf_op jit(solution)/shard_map/ppermute | solution.py:175
  32.2 11.3 %copy-start.3 = (bf16[16,12,8,8,128]{4,3,2,1,0:T(8,128)(2,1)S(1)}, bf16[16,12,8,8,128]{4,3,2,1,0:T(8,128)(2,1)}, u32[]{:S(2)}) copy-start(bf16[16,12,8,8,128]{4,3,2,1,0:T(8,128)(2,1)} %get-tuple-element.10) | copy-start | bytes 9437188
  46.4 80.1 %all-to-all-start.1 = ((bf16[16,102,8,128]{3,2,1,0:T(8,128)(2,1)}), bf16[16,102,8,128]{3,2,1,0:T(8,128)(2,1)S(1)}, u32[]{:S(2)}, u32[]{:S(2)}) async-start(bf16[16,102,8,128]{3,2,1,0:T(8,128)(2,1)} %pad_maximum_fusion), calls=%async_computation.1 | async-start | bytes 6684672 | tf_op jit(solution)/shard_map/all_to_all | solution.py:249
  126.5 142.0 %copy-start.2 = (bf16[16,102,8,128]{3,2,1,0:T(8,128)(2,1)}, bf16[16,102,8,128]{3,2,1,0:T(8,128)(2,1)S(1)}, u32[]{:S(2)}) copy-start(bf16[16,102,8,128]{3,2,1,0:T(8,128)(2,1)S(1)} %all-to-all-done.1.z_ref) | copy-start | bytes 10027012
  268.5 76.4 %all-to-all-start = ((bf16[16,96,8,128]{3,2,1,0:T(8,128)(2,1)}), bf16[16,96,8,128]{3,2,1,0:T(8,128)(2,1)}, u32[]{:S(2)}, u32[]{:S(2)}) async-start(bf16[16,96,8,128]{3,2,1,0:T(8,128)(2,1)} %bitcast.42), calls=%async_computation | async-start | bytes 6291456 | tf_op jit(solution)/shard_map/all_to_all | solution.py:249
  276.1 4.5 %copy-start.5 = (s32[192]{0:T(256)S(1)}, s32[192]{0:T(256)}, u32[]{:S(2)}) copy-start(s32[192]{0:T(256)} %order_ref.5) | copy-start | bytes 2308
  276.1 4.5 %slice-start = ((bf16[16,102,8,128]{3,2,1,0:T(8,128)(2,1)}), bf16[16,6,8,128]{3,2,1,0:T(8,128)(2,1)S(1)}, s32[]{:S(2)}) async-start(bf16[16,102,8,128]{3,2,1,0:T(8,128)(2,1)} %copy-done.2), calls=%async_computation.3 | async-start | bytes 393216 | tf_op jit(solution)/shard_map/slice | solution.py:250
  344.9 19.8 %copy-start.1 = (f32[16,16]{1,0:T(8,128)S(1)}, f32[16,16]{1,0:T(8,128)}, u32[]{:S(2)}) copy-start(f32[16,16]{1,0:T(8,128)} %param.11) | copy-start | bytes 3076
